TPU v7x, 32 devices: a whole 2x2x4 slice. The times are simulated.
32 devices in a mesh: seq: 16 (over z, y, x), head: 2 (over core).
Axes of the slice: x: 2, y: 2, z: 4, core: 2. Of those that a mesh axis runs over, the one named last changes fastest.
Arguments:
- queries: bfloat16 [2048, 64, 512], P('seq', 'head'), may hold values from -1000 to 1000
- cotangent: bfloat16 [2048, 64, 512], P('seq', 'head'), may hold values from -6 to 6
- window_kv: bfloat16 [2048, 512], P('seq'), may hold values from -6 to 6
- context: bfloat16 [4096, 512], P(('seq', 'head')), may hold values from -6 to 6
- pool_weight: float32 [128, 512], replicated, may hold values from -0.5 to 0.5
Outputs:
- attn_out: bfloat16 [2048, 64, 512], P('seq', 'head')
- grad_queries: bfloat16 [2048, 64, 512], P('seq', 'head')
- grad_context: float32 [4096, 512], P(('seq', 'head'))
All inputs are finite; a program needn't handle non-finite values.
Results may differ from a plain program's by a relative error of at most 0.0074.
Values may be sent and summed in bfloat16 or wider, within the bound.
No kernel may reach another device: no remote copies, remote signals or barrier semaphores. Data moves between devices by JAX's collectives and lax.ppermute only.
A program may use at most 64 MiB of HBM per device.

v0:
```python
import functools

import jax
import jax.numpy as jnp
from jax import lax
from jax.experimental import pallas as pl
from jax.experimental.pallas import tpu as pltpu
from jax.sharding import PartitionSpec as P

POOL = 128
WINDOW = 128
TILE = 16
AXES = ("seq", "head")
LOG2E = 1.4426950408889634
NT = (((1,), (1,)), ((), ()))
TN = (((0,), (0,)), ((), ()))


def whole(shape):
    return pl.BlockSpec(shape, lambda *_: (0,) * len(shape))


def pool_kernel(context_ref, weight_ref, pooled_ref, send_ref):
    rows = pooled_ref.shape[0]
    copies = send_ref.shape[0] // rows
    parts = []
    for block in range(rows):
        entries = context_ref[pl.ds(block * POOL, POOL), :].astype(jnp.float32)
        parts.append(jnp.sum(entries * weight_ref[...], axis=0, keepdims=True))
    pooled = parts[0] if rows == 1 else jnp.concatenate(parts, 0)
    pooled_ref[...] = pooled
    inverse = lax.rsqrt(jnp.mean(pooled * pooled, -1, keepdims=True) + 1e-06)
    normed = pooled * inverse
    if rows == 1:
        spread = jnp.broadcast_to(normed, send_ref.shape)
    else:
        spread = jnp.concatenate([normed] * copies, 0)
    send_ref[...] = spread.astype(jnp.bfloat16)


def finish_kernel(parts_ref, pooled_ref, weight_ref, out_ref):
    rows, width = pooled_ref.shape
    copies = parts_ref.shape[0] // rows
    parts = parts_ref[...]
    if rows == 1:
        total = jnp.sum(parts, axis=0, keepdims=True)
    else:
        total = jnp.sum(parts.reshape(copies, rows, width), axis=0)
    pooled = pooled_ref[...]
    inverse = lax.rsqrt(jnp.mean(pooled * pooled, -1, keepdims=True) + 1e-06)
    normed = pooled * inverse
    grad = inverse * (total - normed * jnp.mean(total * normed, -1, keepdims=True))
    for block in range(rows):
        out_ref[pl.ds(block * POOL, POOL), :] = weight_ref[...] * grad[block : block + 1, :]


def fill_keys(step, comp_ref, prev_ref, cur_ref, window_ref, keys_ref):
    count = comp_ref.shape[0]

    @pl.when(step == 0)
    def _():
        window_ref[pl.ds(0, WINDOW), :] = prev_ref[...]
        window_ref[pl.ds(WINDOW, cur_ref.shape[0]), :] = cur_ref[...]
        keys_ref[pl.ds(0, count), :] = comp_ref[...]

    start = pl.multiple_of(step * TILE, TILE)
    keys_ref[pl.ds(count, TILE + WINDOW), :] = window_ref[pl.ds(start, TILE + WINDOW), :]


def score_kernel(heads, first_ref, q_ref, c_ref, comp_ref, prev_ref, cur_ref, p_ref, g_ref, sum_ref, window_ref, keys_ref):
    step = pl.program_id(0)
    count = comp_ref.shape[0]
    rows, width = q_ref.shape
    factor = width ** (-0.5)
    fill_keys(step, comp_ref, prev_ref, cur_ref, window_ref, keys_ref)
    keys = keys_ref[...]
    chunk = min(256, rows)
    slab = TILE + WINDOW
    low = jnp.where(first_ref[0] > 0, WINDOW - step * TILE, 0)
    total = jnp.zeros(sum_ref.shape, jnp.float32)
    for at in range(0, rows, chunk):
        q = q_ref[pl.ds(at, chunk), :]
        c = c_ref[pl.ds(at, chunk), :]
        scores = lax.dot_general(keys, q, NT, preferred_element_type=jnp.float32)
        grads = lax.dot_general(keys, c, NT, preferred_element_type=jnp.float32)
        key = lax.broadcasted_iota(jnp.int32, (slab, chunk), 0)
        token = (lax.broadcasted_iota(jnp.int32, (slab, chunk), 1) + at) // heads
        valid = (key > token) & (key <= token + WINDOW) & (key >= low)
        scores = jnp.concatenate([scores[:count], jnp.where(valid, scores[count:], -1e30)], 0)
        peak = jnp.max(scores, 0, keepdims=True)
        weights = jnp.exp2((scores - peak) * (factor * LOG2E))
        probs = weights * (1.0 / jnp.sum(weights, 0, keepdims=True))
        half = probs.astype(jnp.bfloat16)
        delta = jnp.sum(half.astype(jnp.float32) * grads, 0, keepdims=True)
        slope = (probs * (grads - delta)).astype(jnp.bfloat16)
        p_ref[0, :, pl.ds(at, chunk)] = half
        g_ref[0, :, pl.ds(at, chunk)] = slope
        total += jnp.dot(half[:count], c, preferred_element_type=jnp.float32)
        total += factor * jnp.dot(slope[:count], q, preferred_element_type=jnp.float32)

    @pl.when(step == 0)
    def _():
        sum_ref[...] = total

    @pl.when(step > 0)
    def _():
        sum_ref[...] += total


def output_kernel(p_ref, g_ref, comp_ref, prev_ref, cur_ref, out_ref, grad_ref, window_ref, keys_ref):
    step = pl.program_id(0)
    fill_keys(step, comp_ref, prev_ref, cur_ref, window_ref, keys_ref)
    rows, width = out_ref.shape
    factor = width ** (-0.5)
    keys = keys_ref[...]
    chunk = min(256, rows)
    for at in range(0, rows, chunk):
        half = p_ref[0, :, pl.ds(at, chunk)]
        slope = g_ref[0, :, pl.ds(at, chunk)]
        out = lax.dot_general(half, keys, TN, preferred_element_type=jnp.float32)
        out_ref[pl.ds(at, chunk), :] = out.astype(jnp.bfloat16)
        grad = lax.dot_general(slope, keys, TN, preferred_element_type=jnp.float32)
        grad_ref[pl.ds(at, chunk), :] = (grad * factor).astype(jnp.bfloat16)


def local(queries, cotangent, window_kv, context, pool_weight):
    tokens, heads, width = queries.shape
    pool_rows = context.shape[0] // POOL
    devices = lax.axis_size("seq") * lax.axis_size("head")
    count = devices * pool_rows
    rows = tokens * heads
    steps = tokens // TILE
    block = TILE * heads
    slab = count + TILE + WINDOW

    pooled, send = pl.pallas_call(
        pool_kernel,
        out_shape=(
            jax.ShapeDtypeStruct((pool_rows, width), jnp.float32),
            jax.ShapeDtypeStruct((count, width), jnp.bfloat16),
        ),
        name="pool",
    )(context, pool_weight)
    comp = lax.all_to_all(send, AXES, 0, 0, tiled=True)
    size = lax.axis_size("seq")
    prev = lax.ppermute(window_kv[-WINDOW:], "seq", [(i, i + 1) for i in range(size - 1)])
    first = (lax.axis_index("seq") == 0).astype(jnp.int32).reshape(1)

    q = queries.reshape(rows, width)
    c = cotangent.reshape(rows, width)
    tile = pl.BlockSpec((block, width), lambda i: (i, 0))
    probs = pl.BlockSpec((1, slab, block), lambda i: (i, 0, 0))
    keys = [whole((count, width)), whole((WINDOW, width)), whole((tokens, width))]
    scratch = [
        pltpu.VMEM((WINDOW + tokens, width), jnp.bfloat16),
        pltpu.VMEM((slab, width), jnp.bfloat16),
    ]
    kept = jax.ShapeDtypeStruct((steps, slab, block), jnp.bfloat16)
    half, slope, grad_comp = pl.pallas_call(
        functools.partial(score_kernel, heads),
        grid=(steps,),
        in_specs=[pl.BlockSpec(memory_space=pltpu.SMEM), tile, tile, *keys],
        out_specs=(probs, probs, whole((count, width))),
        out_shape=(kept, kept, jax.ShapeDtypeStruct((count, width), jnp.float32)),
        scratch_shapes=scratch,
        cost_estimate=pl.CostEstimate(
            flops=4 * rows * slab * width + 4 * rows * count * width,
            bytes_accessed=4 * rows * (width + slab),
            transcendentals=rows * slab,
        ),
        name="score",
    )(first, q, c, comp, prev, window_kv)
    parts = lax.all_to_all(grad_comp, AXES, 0, 0, tiled=True)
    out, grad = pl.pallas_call(
        output_kernel,
        grid=(steps,),
        in_specs=[probs, probs, *keys],
        out_specs=(tile, tile),
        out_shape=(jax.ShapeDtypeStruct((rows, width), jnp.bfloat16),) * 2,
        scratch_shapes=scratch,
        cost_estimate=pl.CostEstimate(
            flops=4 * rows * slab * width,
            bytes_accessed=4 * rows * (width + slab),
            transcendentals=0,
        ),
        name="outputs",
    )(half, slope, comp, prev, window_kv)
    grad_context = pl.pallas_call(
        finish_kernel,
        out_shape=jax.ShapeDtypeStruct(context.shape, jnp.float32),
        name="finish",
    )(parts, pooled, pool_weight)
    return out.reshape(queries.shape), grad.reshape(queries.shape), grad_context


def solution(mesh):
    in_specs = (
        P("seq", "head", None),
        P("seq", "head", None),
        P("seq", None),
        P(("seq", "head"), None),
        P(),
    )
    out_specs = (P("seq", "head", None), P("seq", "head", None), P(("seq", "head"), None))
    return jax.shard_map(local, mesh=mesh, in_specs=in_specs, out_specs=out_specs, check_vma=False)
```

profile of v0, /device:TPU:0, one launch (start us, length us, event | category | flops | bytes accessed | tf_op | source)
XLA Modules:
  0.0 50.4 jit_solution(7430073994691621443)
XLA Ops:
  0.6 4.9 %collective-permute-start = (bf16[128,512]{1,0:T(8,128)(2,1)}, bf16[128,512]{1,0:T(8,128)(2,1)S(1)}, u32[]{:S(2)}, u32[]{:S(2)}) collective-permute-start(bf16[128,512]{1,0:T(8,128)(2,1)} %cur_ref.3), channel_id=1, source_target_pairs={{0,2},{2,4},{4,6},{6,8},{8,10},{10,12},{12,14},{14,16},{16,18},{18... | collective-permute-start | bytes 393224 | tf_op jit(solution)/shard_map/ppermute | solution.py:146
  5.5 1.8 %pool.1 = (f32[1,512]{1,0:T(1,128)}, bf16[32,512]{1,0:T(8,128)(2,1)}) custom-call(bf16[128,512]{1,0:T(8,128)(2,1)} %context_ref.1, f32[128,512]{1,0:T(8,128)} %weight_ref.3), custom_call_target="tpu_custom_call" | custom-call | tf_op jit(solution)/shard_map/pool/pallas_call | solution.py:136
  7.3 0.5 %broadcast = bf16[]{:T(256)} broadcast(bf16[]{:T(256)} %constant.8), dimensions={} | broadcast | bytes 4 | tf_op jit(solution)/shard_map/all_to_all | solution.py:144
  7.8 1.4 %reduce = bf16[32,512]{1,0:T(8,128)(2,1)S(1)} reduce(bf16[32,1,512]{2,0,1:T(8,128)(2,1)} %bitcast.19, bf16[]{:T(256)} %broadcast), dimensions={1}, to_apply=%copy.10.reduce_sub_computation | reduce | bytes 65538 | tf_op jit(solution)/shard_map/all_to_all | solution.py:144
  9.2 0.6 %reshape.35 = bf16[32,2,256]{2,1,0:T(2,128)(2,1)} reshape(bf16[32,512]{1,0:T(8,128)(2,1)S(1)} %reduce) | data formatting | bytes 65536
  9.8 4.9 %all-to-all-start = ((bf16[32,2,256]{2,1,0:T(2,128)(2,1)}), bf16[32,2,256]{2,1,0:T(2,128)(2,1)S(1)}, u32[]{:S(2)}, u32[]{:S(2)}) async-start(bf16[32,2,256]{2,1,0:T(2,128)(2,1)} %reshape.35), calls=%async_computation | async-start | bytes 65536 | tf_op jit(solution)/shard_map/all_to_all | solution.py:144
  14.8 7.2 %all-to-all-done = bf16[32,2,256]{2,1,0:T(2,128)(2,1)S(1)} async-done(((bf16[32,2,256]{2,1,0:T(2,128)(2,1)}), bf16[32,2,256]{2,1,0:T(2,128)(2,1)S(1)}, u32[]{:S(2)}, u32[]{:S(2)}) %all-to-all-start) | async-done | bytes 32800 | tf_op jit(solution)/shard_map/all_to_all | solution.py:144
  22.1 0.6 %copy.17 = bf16[32,1,512]{2,0,1:T(8,128)(2,1)} copy(bf16[32,1,512]{2,1,0:T(2,128)(2,1)S(1)} %reshape.36) | data formatting | bytes 65536
  22.7 0.0 collective-permute-done.prev_ref
  22.7 0.0 copy-start
  22.7 0.7 %copy-done = bf16[128,512]{1,0:T(8,128)(2,1)} copy-done((bf16[128,512]{1,0:T(8,128)(2,1)}, bf16[128,512]{1,0:T(8,128)(2,1)S(1)}, u32[]{:S(2)}) %copy-start) | copy-done | bytes 131096
  23.3 11.6 %score.1 = (bf16[8,176,512]{2,1,0:T(8,128)(2,1)}, bf16[8,176,512]{2,1,0:T(8,128)(2,1)}, f32[32,512]{1,0:T(8,128)}) custom-call(s32[1]{0:T(128)} %bitcast.first_ref, bf16[4096,512]{1,0:T(8,128)(2,1)} %bitcast.13, bf16[4096,512]{1,0:T(8,128)(2,1)} %bitcast.14, bf16[32,512]{1,0:T(8,128)(2,1)} %bitcast.16, bf16[128,512]{1,0:T(8,128)(2,1)} %copy-done, ...), custom_call_target="tpu_custom_call" | custom-call | flops 1744830464 | bytes 11272192 | tf_op jit(solution)/shard_map/score/pallas_call | solution.py:159
  35.0 1.5 %copy.11 = f32[32,1,512]{2,1,0:T(1,128)} copy(f32[32,1,512]{2,0,1:T(8,128)} %bitcast.18) | data formatting | bytes 131072 | tf_op jit(solution)/shard_map/all_to_all | solution.py:173
  36.5 2.6 %all-to-all-start.1 = ((f32[32,1,512]{2,1,0:T(1,128)}), f32[32,1,512]{2,1,0:T(1,128)S(1)}, u32[]{:S(2)}, u32[]{:S(2)}) async-start(f32[32,1,512]{2,1,0:T(1,128)} %copy.11), calls=%async_computation.1 | async-start | bytes 131072 | tf_op jit(solution)/shard_map/all_to_all | solution.py:173
  39.1 8.8 %outputs.1 = (bf16[4096,512]{1,0:T(8,128)(2,1)}, bf16[4096,512]{1,0:T(8,128)(2,1)}) custom-call(bf16[8,176,512]{2,1,0:T(8,128)(2,1)} %get-tuple-element.11.p_ref, bf16[8,176,512]{2,1,0:T(8,128)(2,1)} %get-tuple-element.12.g_ref, bf16[32,512]{1,0:T(8,128)(2,1)} %bitcast.17, bf16[128,512]{1,0:T(8,128)(2,1)} %copy-done, bf16[128,512]{1,0:T(8,128)(2,1)} %cur_ref.3), custom_call_target="tpu_custom_call" | custom-call | flops 1476395008 | bytes 11272192 | tf_op jit(solution)/shard_map/outputs/pallas_call | solution.py:174
  47.9 0.0 all-to-all-done.1
  47.9 0.6 %copy.16 = f32[32,1,512]{2,0,1:T(8,128)} copy(f32[32,1,512]{2,1,0:T(1,128)S(1)} %all-to-all-done.1) | data formatting | bytes 131072
  48.6 1.9 %finish.1 = f32[128,512]{1,0:T(8,128)} custom-call(f32[32,512]{1,0:T(8,128)} %bitcast.15, f32[1,512]{1,0:T(1,128)} %get-tuple-element.16.pooled_ref, f32[128,512]{1,0:T(8,128)} %weight_ref.3), custom_call_target="tpu_custom_call" | custom-call | tf_op jit(solution)/shard_map/finish/pallas_call | solution.py:188
  (1 shorter events, 0.0 us)
Async XLA Ops:
  0.6 22.0 %collective-permute-start = (bf16[128,512]{1,0:T(8,128)(2,1)}, bf16[128,512]{1,0:T(8,128)(2,1)S(1)}, u32[]{:S(2)}, u32[]{:S(2)}) collective-permute-start(bf16[128,512]{1,0:T(8,128)(2,1)} %cur_ref.3), channel_id=1, source_target_pairs={{0,2},{2,4},{4,6},{6,8},{8,10},{10,12},{12,14},{14,16},{16,18},{18... | collective-permute-start | bytes 393224 | tf_op jit(solution)/shard_map/ppermute | solution.py:146
  9.8 12.2 %all-to-all-start = ((bf16[32,2,256]{2,1,0:T(2,128)(2,1)}), bf16[32,2,256]{2,1,0:T(2,128)(2,1)S(1)}, u32[]{:S(2)}, u32[]{:S(2)}) async-start(bf16[32,2,256]{2,1,0:T(2,128)(2,1)} %reshape.35), calls=%async_computation | async-start | bytes 65536 | tf_op jit(solution)/shard_map/all_to_all | solution.py:144
  22.7 0.7 %copy-start = (bf16[128,512]{1,0:T(8,128)(2,1)}, bf16[128,512]{1,0:T(8,128)(2,1)S(1)}, u32[]{:S(2)}) copy-start(bf16[128,512]{1,0:T(8,128)(2,1)S(1)} %collective-permute-done.prev_ref) | copy-start | bytes 393220
  36.5 11.4 %all-to-all-start.1 = ((f32[32,1,512]{2,1,0:T(1,128)}), f32[32,1,512]{2,1,0:T(1,128)S(1)}, u32[]{:S(2)}, u32[]{:S(2)}) async-start(f32[32,1,512]{2,1,0:T(1,128)} %copy.11), calls=%async_computation.1 | async-start | bytes 131072 | tf_op jit(solution)/shard_map/all_to_all | solution.py:173
where the time goes:
time: 51.2 us; the launch traced here: 50.4 us
  Pallas kernels  24.1 us (47%)
  starting transfers between devices  12.4 us (24%)
  waiting for transfers between devices  7.25 us (14%)
  local copies, waits for them, and re-layouts  4.62 us (9%)
  other arithmetic  1.41 us (3%)
  between operations  0.67 us (1%)
    pallas_call x1, Pallas kernels, local(): pl.pallas_call(functools.partial(score_kernel, heads), grid=(steps,), in_...  11.6 us
    pallas_call x1, Pallas kernels, local(): pl.pallas_call(output_kernel, grid=(steps,), in_specs=[probs, probs, *key...  8.83 us
    all_to_all x1, waiting for transfers between devices, local(): comp = lax.all_to_all(send, AXES, 0, 0, tiled=True)  7.25 us
    all_to_all x1, starting transfers between devices, local(): comp = lax.all_to_all(send, AXES, 0, 0, tiled=True)  4.92 us
    ppermute x1, starting transfers between devices, local(): lax.ppermute(window_kv[-WINDOW:], 'seq', [(i, i + 1) for i in range(size...  4.88 us
    unnamed x6, local copies, waits for them, and re-layouts  2.57 us
    all_to_all x1, starting transfers between devices, local(): parts = lax.all_to_all(grad_comp, AXES, 0, 0, tiled=True)  2.56 us
    pallas_call x1, Pallas kernels, local(): pl.pallas_call(finish_kernel, out_shape=jax.ShapeDtypeStruct(context.shap...  1.89 us
  transfers between devices with their start and end apart: 3, of which 1 were waited for; matrix products, arithmetic and copies ran while one was open for 6% of the time, Pallas kernels for 21%

commit v1 on v0

v1 whole, which is shorter than its diff:
```python
import functools

import jax
import jax.numpy as jnp
from jax import lax
from jax.experimental import pallas as pl
from jax.experimental.pallas import tpu as pltpu
from jax.sharding import PartitionSpec as P


POOL = 128
WINDOW = 128
LANES = 128
GROUP = 2
TILE = 16
AXES = ("seq", "head")
LOG2E = 1.4426950408889634
MIB = 1 << 20
NT = (((1,), (1,)), ((), ()))
TN = (((0,), (0,)), ((), ()))
HBM = pl.BlockSpec(memory_space=pltpu.HBM)
VMEM = pl.BlockSpec(memory_space=pltpu.VMEM)
SMEM = pl.BlockSpec(memory_space=pltpu.SMEM)


def hbm(value):
    return pltpu.with_memory_space_constraint(value, pltpu.HBM)


def vmem(value):
    return pltpu.with_memory_space_constraint(value, pltpu.VMEM)


def pool_kernel(context_hbm, weight_hbm, pooled_ref, send_ref, context_ref, weight_ref, sem):
    blocks, width = pooled_ref.shape
    copies = (
        pltpu.make_async_copy(context_hbm, context_ref, sem.at[0]),
        pltpu.make_async_copy(weight_hbm, weight_ref, sem.at[1]),
    )
    for copy in copies:
        copy.start()
    for copy in copies:
        copy.wait()
    for block in range(blocks):
        entries = context_ref[pl.ds(block * POOL, POOL), :].astype(jnp.float32)
        pooled = jnp.sum(entries * weight_ref[...], axis=0, keepdims=True)
        pooled_ref[pl.ds(block, 1), :] = pooled
        normed = pooled * lax.rsqrt(jnp.mean(pooled * pooled, -1, keepdims=True) + 1e-06)
        lines = jnp.concatenate([normed[:, at : at + LANES] for at in range(0, width, LANES)], 0)
        if blocks == 1:
            send_ref[...] = jnp.broadcast_to(lines[None], send_ref.shape)
        else:
            for peer in range(send_ref.shape[0] // blocks):
                send_ref[peer * blocks + block] = lines


def finish_kernel(parts_ref, pooled_ref, weight_ref, out_ref):
    blocks, _ = pooled_ref.shape
    count, lines, lanes = parts_ref.shape
    total = jnp.sum(parts_ref[...].reshape(count // blocks, blocks, lines, lanes), 0)
    for block in range(blocks):
        grad = jnp.concatenate([total[block, j : j + 1] for j in range(lines)], 1)
        pooled = pooled_ref[pl.ds(block, 1), :]
        inverse = lax.rsqrt(jnp.mean(pooled * pooled, -1, keepdims=True) + 1e-06)
        normed = pooled * inverse
        grad = inverse * (grad - normed * jnp.mean(grad * normed, -1, keepdims=True))
        out_ref[pl.ds(block * POOL, POOL), :] = weight_ref[...] * grad


def fill_keys(comp_ref, prev_ref, window_ref, *keys_refs):
    count, lines, lanes = comp_ref.shape
    window_ref[pl.ds(0, WINDOW), :] = prev_ref[...]
    for line in range(lines):
        piece = comp_ref[:, line, :].astype(jnp.bfloat16)
        for keys_ref in keys_refs:
            keys_ref[pl.ds(0, count), pl.ds(line * lanes, lanes)] = piece


def score_kernel(
    heads, first_ref, q_hbm, c_hbm, comp_ref, prev_ref, cur_hbm, p_ref, g_ref, sum_ref,
    q_ref, c_ref, window_ref, keys_ref, total_ref, sem, cur_sem,
):
    count, lines, lanes = comp_ref.shape
    rows, width = q_ref.shape
    part = TILE * heads
    group = min(GROUP, p_ref.shape[0])
    block = part * group
    steps = rows // block
    slab = TILE * group + WINDOW
    factor = width ** (-0.5)

    def fetch(step):
        span = pl.ds(pl.multiple_of(step * block, block), block)
        return (
            pltpu.make_async_copy(q_hbm.at[span], q_ref.at[span], sem.at[0, step]),
            pltpu.make_async_copy(c_hbm.at[span], c_ref.at[span], sem.at[1, step]),
        )

    copy_cur = pltpu.make_async_copy(cur_hbm, window_ref.at[pl.ds(WINDOW, cur_hbm.shape[0])], cur_sem)
    copy_cur.start()
    for step in range(steps):
        for copy in fetch(step):
            copy.start()
    fill_keys(comp_ref, prev_ref, window_ref, keys_ref)
    total_ref[...] = jnp.zeros_like(total_ref)
    copy_cur.wait()

    @pl.loop(0, steps)
    def _(step):
        start = pl.multiple_of(step * (TILE * group), TILE * group)
        keys_ref[pl.ds(count, slab), :] = window_ref[pl.ds(start, slab), :]
        for copy in fetch(step):
            copy.wait()
        keys = keys_ref[...]
        span = pl.ds(pl.multiple_of(step * block, block), block)
        q = q_ref[span, :]
        c = c_ref[span, :]
        scores = lax.dot_general(keys, q, NT, preferred_element_type=jnp.float32)
        grads = lax.dot_general(keys, c, NT, preferred_element_type=jnp.float32)
        key = lax.broadcasted_iota(jnp.int32, (slab, block), 0)
        token = lax.broadcasted_iota(jnp.int32, (slab, block), 1) // heads
        low = jnp.where(first_ref[0] > 0, WINDOW - start, 0)
        valid = (key > token) & (key <= token + WINDOW) & (key >= low)
        scores = jnp.concatenate([scores[:count], jnp.where(valid, scores[count:], -1e30)], 0)
        peak = jnp.max(scores, 0, keepdims=True)
        weights = jnp.exp2((scores - peak) * (factor * LOG2E))
        probs = weights * (1.0 / jnp.sum(weights, 0, keepdims=True))
        half = probs.astype(jnp.bfloat16)
        delta = jnp.sum(half.astype(jnp.float32) * grads, 0, keepdims=True)
        slope = (probs * (grads - delta)).astype(jnp.bfloat16)
        for ref, value in ((p_ref, half), (g_ref, slope)):
            for index in range(group):
                columns = slice(index * part, (index + 1) * part)
                first = count + index * TILE
                ref[step * group + index, pl.ds(0, count), :] = value[:count, columns]
                window = value[first : first + TILE + WINDOW, columns]
                ref[step * group + index, pl.ds(count, TILE + WINDOW), :] = window
        total = jnp.dot(half[:count], c, preferred_element_type=jnp.float32)
        total += factor * jnp.dot(slope[:count], q, preferred_element_type=jnp.float32)
        total_ref[...] += total

    for line in range(lines):
        sum_ref[:, line, :] = total_ref[:, pl.ds(line * lanes, lanes)]


def output_kernel(
    p_ref, g_ref, comp_ref, prev_ref, cur_hbm, out_hbm, grad_hbm,
    out_ref, grad_ref, window_ref, keys_refs, sem, cur_sem,
):
    steps, _, block = p_ref.shape
    count = comp_ref.shape[0]
    factor = out_ref.shape[1] ** (-0.5)
    unroll = 2 if steps % 2 == 0 else 1

    def flush(step):
        rows = pl.ds(pl.multiple_of(step * block, block), block)
        return (
            pltpu.make_async_copy(out_ref.at[rows], out_hbm.at[rows], sem.at[0, step]),
            pltpu.make_async_copy(grad_ref.at[rows], grad_hbm.at[rows], sem.at[1, step]),
        )

    copy_cur = pltpu.make_async_copy(cur_hbm, window_ref.at[pl.ds(WINDOW, cur_hbm.shape[0])], cur_sem)
    copy_cur.start()
    fill_keys(comp_ref, prev_ref, window_ref, keys_refs.at[0], keys_refs.at[1])
    copy_cur.wait()

    @pl.loop(0, steps // unroll)
    def _(turn):
        for slot in range(unroll):
            step = turn * unroll + slot
            start = pl.multiple_of(step * TILE, TILE)
            keys_refs[slot, pl.ds(count, TILE + WINDOW), :] = window_ref[pl.ds(start, TILE + WINDOW), :]
            keys = keys_refs[slot]
            rows = pl.ds(pl.multiple_of(step * block, block), block)
            out = lax.dot_general(p_ref[step], keys, TN, preferred_element_type=jnp.float32)
            out_ref[rows, :] = out.astype(jnp.bfloat16)
            grad = lax.dot_general(g_ref[step], keys, TN, preferred_element_type=jnp.float32)
            grad_ref[rows, :] = (grad * factor).astype(jnp.bfloat16)
        for slot in range(unroll):
            for copy in flush(turn * unroll + slot):
                copy.start()

    for step in range(steps):
        for copy in flush(step):
            copy.wait()


def local(queries, cotangent, window_kv, context, pool_weight):
    tokens, heads, width = queries.shape
    blocks = context.shape[0] // POOL
    size = lax.axis_size("seq")
    count = size * lax.axis_size("head") * blocks
    rows = tokens * heads
    steps = tokens // TILE
    block = TILE * heads
    slab = count + TILE + WINDOW
    lines = width // LANES

    packed = jax.ShapeDtypeStruct((count, lines, LANES), jnp.float32)
    pooled, send = pl.pallas_call(
        pool_kernel,
        in_specs=[HBM, HBM],
        out_specs=(VMEM, VMEM),
        out_shape=(jax.ShapeDtypeStruct((blocks, width), jnp.float32), packed),
        scratch_shapes=[
            pltpu.VMEM(context.shape, context.dtype),
            pltpu.VMEM(pool_weight.shape, pool_weight.dtype),
            pltpu.SemaphoreType.DMA((2,)),
        ],
        name="pool",
        compiler_params=pltpu.CompilerParams(vmem_limit_bytes=8 * MIB),
    )(hbm(context), hbm(pool_weight))
    comp = lax.all_to_all(send, AXES, 0, 0, tiled=True)
    prev = lax.ppermute(window_kv[-WINDOW:], "seq", [(i, i + 1) for i in range(size - 1)])
    first = (lax.axis_index("seq") == 0).astype(jnp.int32).reshape(1)

    q = hbm(queries.reshape(rows, width))
    c = hbm(cotangent.reshape(rows, width))
    cur = hbm(window_kv)
    full = pltpu.VMEM((rows, width), jnp.bfloat16)
    kept = pltpu.VMEM((steps, slab, block), jnp.bfloat16)
    group = min(GROUP, steps)
    window = pltpu.VMEM((WINDOW + tokens, width), jnp.bfloat16)
    wide = pltpu.VMEM((count + TILE * group + WINDOW, width), jnp.bfloat16)
    total = pltpu.VMEM((count, width), jnp.float32)
    params = pltpu.CompilerParams(vmem_limit_bytes=32 * MIB)
    half, slope, grad_comp = pl.pallas_call(
        functools.partial(score_kernel, heads),
        in_specs=[SMEM, HBM, HBM, VMEM, VMEM, HBM],
        out_specs=(VMEM, VMEM, VMEM),
        out_shape=(kept, kept, packed),
        scratch_shapes=[full, full, window, wide, total, pltpu.SemaphoreType.DMA((2, steps // group)), pltpu.SemaphoreType.DMA],
        cost_estimate=pl.CostEstimate(
            flops=4 * rows * slab * width + 4 * rows * count * width,
            bytes_accessed=4 * rows * (width + slab),
            transcendentals=rows * slab,
        ),
        compiler_params=params,
        name="score",
    )(first, q, c, comp, prev, cur)
    parts = lax.all_to_all(grad_comp, AXES, 0, 0, tiled=True)
    out, grad = pl.pallas_call(
        output_kernel,
        in_specs=[VMEM, VMEM, VMEM, VMEM, HBM],
        out_specs=(HBM, HBM),
        out_shape=(jax.ShapeDtypeStruct((rows, width), jnp.bfloat16),) * 2,
        scratch_shapes=[full, full, window, pltpu.VMEM((2, slab, width), jnp.bfloat16), pltpu.SemaphoreType.DMA((2, steps)), pltpu.SemaphoreType.DMA],
        cost_estimate=pl.CostEstimate(
            flops=4 * rows * slab * width,
            bytes_accessed=4 * rows * (width + slab),
            transcendentals=0,
        ),
        compiler_params=params,
        name="outputs",
    )(vmem(half), vmem(slope), comp, prev, cur)
    grad_context = pl.pallas_call(
        finish_kernel,
        out_shape=jax.ShapeDtypeStruct(context.shape, jnp.float32),
        name="finish",
        compiler_params=pltpu.CompilerParams(vmem_limit_bytes=8 * MIB),
    )(parts, pooled, pool_weight)
    return out.reshape(queries.shape), grad.reshape(queries.shape), grad_context


def solution(mesh):
    in_specs = (
        P("seq", "head", None),
        P("seq", "head", None),
        P("seq", None),
        P(("seq", "head"), None),
        P(),
    )
    out_specs = (P("seq", "head", None), P("seq", "head", None), P(("seq", "head"), None))

    return jax.shard_map(local, mesh=mesh, in_specs=in_specs, out_specs=out_specs, check_vma=False)
```

time: 51.2 us -> 39.6 us (0.77)
  Pallas kernels: 24.1 us -> 16.6 us
  local copies, waits for them, and re-layouts: 4.62 us -> 0.01 us
  waiting for transfers between devices: 7.25 us -> 9.56 us
  other arithmetic: 1.41 us -> 0 us
    pallas_call x3, Pallas kernels: 22.2 us -> 15.7 us  [the longest x1 8.61 us: local(): pl.pallas_call(functools.partial(score_kernel, heads), in_specs=[SMEM, HB...]
    unnamed x6 -> x2, local copies, waits for them, and re-layouts: 2.57 us -> 0.01 us
    all_to_all x1, waiting for transfers between devices: 0.01 us -> 2.15 us  [local(): parts = lax.all_to_all(grad_comp, AXES, 0, 0, tiled=True)]
    all_to_all x2 -> x0, local copies, waits for them, and re-layouts: 2.05 us -> none  [the longest x1 1.54 us: local(): parts = lax.all_to_all(grad_comp, AXES, 0, 0, tiled=True)]
    all_to_all x1 -> x0, other arithmetic: 1.41 us -> none  [local(): comp = lax.all_to_all(send, AXES, 0, 0, tiled=True)]
    pallas_call x1, Pallas kernels: 1.89 us -> 0.9 us  [local(): pl.pallas_call(finish_kernel, out_shape=jax.ShapeDtypeStruct(context.shap...]
  transfers between devices with their start and end apart: 3 -> 3, of which waited for: 1 -> 2; matrix products, arithmetic and copies ran while one was open for 6% -> 0% of each run, Pallas kernels for 21% -> 18%
where the time goes in v1:
time: 39.6 us; the launch traced here: 39.3 us
  Pallas kernels  16.6 us (42%)
  starting transfers between devices  12.5 us (32%)
  waiting for transfers between devices  9.56 us (24%)
  between operations  0.69 us (2%)
    pallas_call x1, Pallas kernels, local(): pl.pallas_call(functools.partial(score_kernel, heads), in_specs=[SMEM, HB...  8.61 us
    all_to_all x1, waiting for transfers between devices, local(): comp = lax.all_to_all(send, AXES, 0, 0, tiled=True)  7.4 us
    pallas_call x1, Pallas kernels, local(): pl.pallas_call(output_kernel, in_specs=[VMEM, VMEM, VMEM, VMEM, HBM], out...  5.25 us
    all_to_all x1, starting transfers between devices, local(): comp = lax.all_to_all(send, AXES, 0, 0, tiled=True)  4.93 us
    ppermute x1, starting transfers between devices, local(): lax.ppermute(window_kv[-WINDOW:], 'seq', [(i, i + 1) for i in range(size...  4.88 us
    all_to_all x1, starting transfers between devices, local(): parts = lax.all_to_all(grad_comp, AXES, 0, 0, tiled=True)  2.72 us
    all_to_all x1, waiting for transfers between devices, local(): parts = lax.all_to_all(grad_comp, AXES, 0, 0, tiled=True)  2.15 us
    pallas_call x1, Pallas kernels, local(): pl.pallas_call(pool_kernel, in_specs=[HBM, HBM], out_specs=(VMEM, VMEM),...  1.8 us
  transfers between devices with their start and end apart: 3, of which 2 were waited for; matrix products, arithmetic and copies ran while one was open for 0% of the time, Pallas kernels for 18%

profile of v1, /device:TPU:0, one launch (start us, length us, event | category | flops | bytes accessed | tf_op | source)
XLA Modules:
  0.0 39.3 jit_solution(6176462795358344269)
XLA Ops:
  0.6 4.9 %collective-permute-start = (bf16[128,512]{1,0:T(8,128)(2,1)}, bf16[128,512]{1,0:T(8,128)(2,1)S(1)}, u32[]{:S(2)}, u32[]{:S(2)}) collective-permute-start(bf16[128,512]{1,0:T(8,128)(2,1)} %cur_hbm.3), channel_id=1, source_target_pairs={{0,2},{2,4},{4,6},{6,8},{8,10},{10,12},{12,14},{14,16},{16,18},{18... | collective-permute-start | bytes 393224 | tf_op jit(solution)/shard_map/ppermute | solution.py:214
  5.5 1.8 %pool.1 = (f32[1,512]{1,0:T(1,128)S(1)}, f32[32,4,128]{2,1,0:T(4,128)}) custom-call(bf16[128,512]{1,0:T(8,128)(2,1)} %context_hbm.1, f32[128,512]{1,0:T(8,128)} %weight_ref.1), custom_call_target="tpu_custom_call" | custom-call | tf_op jit(solution)/shard_map/pool/pallas_call | solution.py:200
  7.3 4.9 %all-to-all-start = ((f32[32,4,128]{2,1,0:T(4,128)}), f32[32,4,128]{2,1,0:T(4,128)S(1)}, u32[]{:S(2)}, u32[]{:S(2)}) async-start(f32[32,4,128]{2,1,0:T(4,128)} %get-tuple-element.10), calls=%async_computation | async-start | bytes 131072 | tf_op jit(solution)/shard_map/all_to_all | solution.py:213
  12.3 7.4 %all-to-all-done.comp_ref = f32[32,4,128]{2,1,0:T(4,128)S(1)} async-done(((f32[32,4,128]{2,1,0:T(4,128)}), f32[32,4,128]{2,1,0:T(4,128)S(1)}, u32[]{:S(2)}, u32[]{:S(2)}) %all-to-all-start) | async-done | bytes 65568 | tf_op jit(solution)/shard_map/all_to_all | solution.py:213
  19.7 0.0 collective-permute-done.prev_ref
  19.7 8.6 %score.1 = (bf16[8,176,512]{2,1,0:T(8,128)(2,1)S(1)}, bf16[8,176,512]{2,1,0:T(8,128)(2,1)S(1)}, f32[32,4,128]{2,1,0:T(4,128)}) custom-call(s32[1]{0:T(128)} %bitcast.first_ref, bf16[4096,512]{1,0:T(8,128)(2,1)} %bitcast.5, bf16[4096,512]{1,0:T(8,128)(2,1)} %bitcast.6, f32[32,4,128]{2,1,0:T(4,128)S(1)} %all-to-all-done.comp_ref, ...), custom_call_target="tpu_custom_call" | custom-call | flops 1744830464 | bytes 11272192 | tf_op jit(solution)/shard_map/score/pallas_call | solution.py:227
  28.3 0.0 copy-start
  28.3 2.7 %all-to-all-start.1 = ((f32[32,4,128]{2,1,0:T(4,128)}), f32[32,4,128]{2,1,0:T(4,128)S(1)}, u32[]{:S(2)}, u32[]{:S(2)}) async-start(f32[32,4,128]{2,1,0:T(4,128)} %get-tuple-element.15), calls=%async_computation.1 | async-start | bytes 131072 | tf_op jit(solution)/shard_map/all_to_all | solution.py:241
  31.0 5.2 %outputs.1 = (bf16[4096,512]{1,0:T(8,128)(2,1)}, bf16[4096,512]{1,0:T(8,128)(2,1)}) custom-call(bf16[8,176,512]{2,1,0:T(8,128)(2,1)S(1)} %get-tuple-element.11.p_ref, bf16[8,176,512]{2,1,0:T(8,128)(2,1)S(1)} %get-tuple-element.12.g_ref, f32[32,4,128]{2,1,0:T(4,128)S(1)} %all-to-all-done.comp_ref, bf16[128,512]{1,0:T(8,128)(2,1)S(1)} %collective-permute-done.prev_ref, ...), custom_call_target="tpu_custom_call" | custom-call | flops 1476395008 | bytes 11272192 | tf_op jit(solution)/shard_map/outputs/pallas_call | solution.py:242
  36.3 2.2 %all-to-all-done.1.parts_ref = f32[32,4,128]{2,1,0:T(4,128)S(1)} async-done(((f32[32,4,128]{2,1,0:T(4,128)}), f32[32,4,128]{2,1,0:T(4,128)S(1)}, u32[]{:S(2)}, u32[]{:S(2)}) %all-to-all-start.1) | async-done | bytes 65568 | tf_op jit(solution)/shard_map/all_to_all | solution.py:241
  38.4 0.0 copy-done
  38.4 0.9 %finish.1 = f32[128,512]{1,0:T(8,128)} custom-call(f32[32,4,128]{2,1,0:T(4,128)S(1)} %all-to-all-done.1.parts_ref, f32[1,512]{1,0:T(1,128)S(1)} %get-tuple-element.16.pooled_ref, f32[128,512]{1,0:T(8,128)S(1)} %copy-done), custom_call_target="tpu_custom_call" | custom-call | tf_op jit(solution)/shard_map/finish/pallas_call | solution.py:256
Async XLA Ops:
  0.6 19.0 %collective-permute-start = (bf16[128,512]{1,0:T(8,128)(2,1)}, bf16[128,512]{1,0:T(8,128)(2,1)S(1)}, u32[]{:S(2)}, u32[]{:S(2)}) collective-permute-start(bf16[128,512]{1,0:T(8,128)(2,1)} %cur_hbm.3), channel_id=1, source_target_pairs={{0,2},{2,4},{4,6},{6,8},{8,10},{10,12},{12,14},{14,16},{16,18},{18... | collective-permute-start | bytes 393224 | tf_op jit(solution)/shard_map/ppermute | solution.py:214
  7.3 12.3 %all-to-all-start = ((f32[32,4,128]{2,1,0:T(4,128)}), f32[32,4,128]{2,1,0:T(4,128)S(1)}, u32[]{:S(2)}, u32[]{:S(2)}) async-start(f32[32,4,128]{2,1,0:T(4,128)} %get-tuple-element.10), calls=%async_computation | async-start | bytes 131072 | tf_op jit(solution)/shard_map/all_to_all | solution.py:213
  28.3 10.2 %copy-start = (f32[128,512]{1,0:T(8,128)S(1)}, f32[128,512]{1,0:T(8,128)}, u32[]{:S(2)}) copy-start(f32[128,512]{1,0:T(8,128)} %weight_ref.1) | copy-start | bytes 786436
  28.3 10.1 %all-to-all-start.1 = ((f32[32,4,128]{2,1,0:T(4,128)}), f32[32,4,128]{2,1,0:T(4,128)S(1)}, u32[]{:S(2)}, u32[]{:S(2)}) async-start(f32[32,4,128]{2,1,0:T(4,128)} %get-tuple-element.15), calls=%async_computation.1 | async-start | bytes 131072 | tf_op jit(solution)/shard_map/all_to_all | solution.py:241
